TPU v7x, 32 devices: a whole 2x2x4 slice. The times are simulated.
32 devices in a mesh: ctx: 8 (over y, x, core), dp: 4 (over z).
Axes of the slice: x: 2, y: 2, z: 4, core: 2. Of those that a mesh axis runs over, the one named last changes fastest.
Arguments:
- query_previous: bfloat16 [4, 1024, 2048], P('dp', 'ctx'), may hold values from -240 to 240
- key_previous: bfloat16 [4, 1024, 512], P('dp', 'ctx'), may hold values from -6 to 6
- value_previous: bfloat16 [4, 1024, 512], P('dp', 'ctx'), may hold values from -6 to 6
- span_order: int32 [16], replicated, may hold values from 0 to 15, each once
- resid: bfloat16 [4, 1024, 4096], P('dp', 'ctx'), may hold values from -6 to 6
- grad_norm: bfloat16 [4, 1024, 4096], P('dp', 'ctx'), may hold values from -3 to 3
- gain: float32 [4096], replicated, may hold values from 0.1 to 1.9
Outputs:
- out_prev: bfloat16 [4, 1024, 2048], P('dp', 'ctx')
- lse_prev: float32 [4, 16, 1024], P('dp', None, 'ctx')
- resid_grad: bfloat16 [4, 1024, 4096], P('dp', 'ctx')
- gain_grad: float32 [4096], replicated
Inputs may be any that keep to these rules, and one draw needn't show every extreme that they name: span_order names each of the 16 spans once; rows c * 64 to (c + 1) * 64 - 1 of a sequence's arrays hold span span_order[c].
All inputs are finite; a program needn't handle non-finite values.
Results may differ from a plain program's by a relative error of at most 0.0055.
Values may be sent and summed in bfloat16 or wider, within the bound.
No kernel may reach another device: no remote copies, remote signals or barrier semaphores. Data moves between devices by JAX's collectives and lax.ppermute only.
A program may use at most 64 MiB of HBM per device.

v0:
```python
import math
import jax
import jax.numpy as jnp
from jax import lax
from jax.sharding import PartitionSpec as P

QUERY_HEADS = 16
KEY_VALUE_HEADS = 4
HEAD_WIDTH = 128


def key_positions(tally_count, span_order, half):
    index = jnp.arange(tally_count, dtype=jnp.int32)
    slot = index // half
    table = slot[:, None] == jnp.arange(span_order.shape[0], dtype=jnp.int32)[None, :]
    chosen = jnp.sum(jnp.where(table, span_order[None, :], 0), axis=1)
    return chosen * half + index % half


def dense_update(query_rows, q_positions, carry, key_rows, value_rows, k_positions):
    top, total, summed = carry
    scores = jnp.einsum(
        "rkgd,skd->kgrs", query_rows, key_rows, preferred_element_type=jnp.float32
    ) * HEAD_WIDTH ** (-0.5)
    mask = (k_positions[None, :] <= q_positions[:, None])[None, None]
    scores = jnp.where(mask, scores, -1e30)
    new_top = jnp.maximum(top, jnp.max(scores, axis=-1))
    weights = jnp.where(mask, jnp.exp(scores - new_top[..., None]), 0.0)
    factor = jnp.exp(top - new_top)
    total = total * factor + jnp.sum(weights, axis=-1)
    probs = weights.astype(jnp.bfloat16)
    added = jnp.einsum("kgrs,skd->rkgd", probs, value_rows, preferred_element_type=jnp.float32)
    summed = summed * jnp.transpose(factor, (2, 0, 1))[..., None] + added
    return (new_top, total, summed)


def update(query_rows, q_positions, carry, key_rows, value_rows, k_positions):
    later = jnp.min(k_positions) > jnp.max(q_positions)
    return lax.cond(
        later,
        lambda state: state,
        lambda state: dense_update(
            query_rows, q_positions, state, key_rows, value_rows, k_positions
        ),
        carry,
    )


def fold_piece(query_rows, q_positions, carry, k_piece, v_piece, span_order, half):
    tally_count = k_piece.shape[1]
    heads = k_piece.shape[2] // HEAD_WIDTH
    key_rows = k_piece[0].reshape(tally_count, heads, HEAD_WIDTH)
    value_rows = v_piece[0].reshape(tally_count, heads, HEAD_WIDTH)
    k_positions = key_positions(tally_count, span_order, half)
    block = math.gcd(tally_count, 512)
    steps = tally_count // block

    def step_fn(state, items):
        return (update(query_rows, q_positions, state, items[0], items[1], items[2]), None)

    carry, unused = lax.scan(
        step_fn,
        carry,
        (
            key_rows.reshape(steps, block, heads, HEAD_WIDTH),
            value_rows.reshape(steps, block, heads, HEAD_WIDTH),
            k_positions.reshape(steps, block),
        ),
    )
    return carry


def blank_state(heads, query_group, row_indices):
    return (
        jnp.full((heads, query_group, row_indices), -1e30, jnp.float32),
        jnp.zeros((heads, query_group, row_indices), jnp.float32),
        jnp.zeros((row_indices, heads, query_group, HEAD_WIDTH), jnp.float32),
    )


def attention(query_previous, key_previous, value_previous, span_order):
    row_indices = query_previous.shape[1]
    half = row_indices // 2
    query_group = QUERY_HEADS // KEY_VALUE_HEADS
    mine = lax.dynamic_slice_in_dim(span_order, 2 * lax.axis_index("ctx"), 2)
    local = jnp.arange(row_indices, dtype=jnp.int32)
    q_positions = jnp.where(local < half, mine[0], mine[1]) * half + local % half
    query_rows = query_previous[0].reshape(row_indices, KEY_VALUE_HEADS, query_group, HEAD_WIDTH)
    top, total, summed = fold_piece(
        query_rows,
        q_positions,
        blank_state(KEY_VALUE_HEADS, query_group, row_indices),
        lax.all_gather(key_previous, "ctx", axis=1, tiled=True),
        lax.all_gather(value_previous, "ctx", axis=1, tiled=True),
        span_order,
        half,
    )
    output = summed / jnp.transpose(total, (2, 0, 1))[..., None]
    out_prev = output.reshape(1, row_indices, QUERY_HEADS * HEAD_WIDTH).astype(jnp.bfloat16)
    lse_prev = (top + jnp.log(total)).reshape(1, QUERY_HEADS, row_indices)
    return (out_prev, lse_prev)


def norm_backward(resid, grad_norm, gain):
    resid_f = resid[0].astype(jnp.float32)
    grad_f = grad_norm[0].astype(jnp.float32)
    inv_rms = 1.0 / jnp.sqrt(jnp.mean(resid_f * resid_f, axis=-1, keepdims=True) + 1e-05)
    normed = resid_f * inv_rms
    partial_grad = jnp.sum(grad_f * normed, axis=0)
    gain_grad = lax.psum(partial_grad, ("ctx", "dp"))
    scaled = gain[None, :] * grad_f
    resid_grad = (
        (scaled - normed * jnp.mean(scaled * normed, axis=-1, keepdims=True)) * inv_rms
    ).astype(jnp.bfloat16)
    return (gain_grad, resid_grad[None])


def per_device(query_previous, key_previous, value_previous, span_order, resid, grad_norm, gain):
    out_prev, lse_prev = attention(query_previous, key_previous, value_previous, span_order)
    gain_grad, resid_grad = norm_backward(resid, grad_norm, gain)
    return (out_prev, lse_prev, resid_grad, gain_grad)


def solution(mesh):
    return jax.shard_map(
        per_device,
        mesh=mesh,
        in_specs=(
            P("dp", "ctx", None),
            P("dp", "ctx", None),
            P("dp", "ctx", None),
            P(),
            P("dp", "ctx", None),
            P("dp", "ctx", None),
            P(),
        ),
        out_specs=(P("dp", "ctx", None), P("dp", None, "ctx"), P("dp", "ctx", None), P()),
        check_vma=False,
    )
```

profile of v0, /device:TPU:1, one launch (start us, length us, event | category | flops | bytes accessed | tf_op | source)
XLA Modules:
  0.0 89.6 jit_solution(13001923617092184318)
XLA Ops:
  7.2 0.7 all-gather.3.cloned.1.call-update
  8.0 0.7 all-gather.5.cloned.1.call-update
  8.7 0.7 dynamic_slice.27
  9.4 0.6 fusion.49
  10.0 1.3 %copy.20 = bf16[1,128,2048]{1,2,0:T(8,128)(2,1)S(1)} copy(bf16[1,128,2048]{2,1,0:T(8,128)(2,1)} %param.11) | data formatting | bytes 1048576 | tf_op args[0]
  11.3 0.3 copy.22
  11.6 0.7 select_reduce_fusion
  12.4 1.5 %fusion.38 = f32[128]{0:T(128)S(1)} fusion(bf16[1,128,4096]{2,1,0:T(8,128)(2,1)} %param.15), kind=kLoop, calls=%fused_computation.45 | loop fusion | flops 1572736 | bytes 1049088 | tf_op jit(solution)/shard_map/reduce_sum | solution.py:107
  13.9 1.9 %fusion.47 = s32[]{:T(128)} fusion(s32[]{:T(128)} %bitcast.11, s32[]{:T(128)} %bitcast.10), kind=kLoop, calls=%fused_computation.69 | loop fusion | flops 1407 | bytes 12 | tf_op jit(solution)/shard_map/while/body/eval_jaxpr/reduce_max | solution.py:38
  15.9 2.4 %fusion.34 = (f32[4096]{0:T(1024)S(1)}, f32[128]{0:T(128)S(1)}) fusion(bf16[1,128,4096]{2,1,0:T(8,128)(2,1)} %param.15, bf16[1,128,4096]{2,1,0:T(8,128)(2,1)} %param.16, f32[128]{0:T(128)S(1)} %add_rsqrt_fusion, f32[4096]{0:T(1024)} %param.17), kind=kLoop, calls=%fused_computation.41 | loop fusion | flops 4190080 | bytes 2130944 | tf_op jit(solution)/shard_map/reduce_sum | solution.py:109
  18.2 42.3 %psum.7 = f32[4096]{0:T(1024)} all-reduce(f32[4096]{0:T(1024)S(1)} %get-tuple-element.291), channel_id=1, replica_groups=mesh['ctx'=8,'dp'=4] {'ctx','dp'}, use_global_device_ids=true, to_apply=%region_12.13 | all-reduce | flops 4096 | bytes 32768 | tf_op jit(solution)/shard_map/psum | solution.py:110
  60.5 1.5 %fusion.37 = bf16[1,128,4096]{2,1,0:T(8,128)(2,1)} fusion(bf16[1,128,4096]{2,1,0:T(8,128)(2,1)S(1)} %copy-done.1, bf16[1,128,4096]{2,1,0:T(8,128)(2,1)S(1)} %copy-done, f32[128]{0:T(128)S(1)} %broadcast_multiply_fusion.1, f32[128]{0:T(128)S(1)} %add_rsqrt_fusion, f32[4096]{0:T(1024)S(1)} %copy-done.3), kind=kLoop, calls=%fused_computation.44 | loop fusion | flops 4194304 | bytes 3163136 | tf_op jit(solution)/shard_map/convert_element_type | solution.py:114
  62.1 1.3 %reshape_reshape_squeeze.6 = bf16[2,512,4,128]{3,2,1,0:T(4,128)(2,1)S(1)} reshape(bf16[1,1024,512]{2,1,0:T(8,128)(2,1)} %all-gather.3.cloned.1.call-done) | data formatting | bytes 2097152 | tf_op jit(solution)/shard_map/reshape;reshape;squeeze | solution.py:65
  63.6 1.3 %reshape_reshape_squeeze.7 = bf16[2,512,4,128]{3,2,1,0:T(4,128)(2,1)S(1)} reshape(bf16[1,1024,512]{2,1,0:T(8,128)(2,1)} %all-gather.5.cloned.1.call-done) | data formatting | bytes 2097152 | tf_op jit(solution)/shard_map/reshape;reshape;squeeze | solution.py:66
  64.9 1.1 %copy.23 = bf16[2,512,4,128]{3,1,2,0:T(8,128)(2,1)} copy(bf16[2,512,4,128]{3,2,1,0:T(4,128)(2,1)S(1)} %reshape_reshape_squeeze.7) | data formatting | bytes 2097152
  66.2 14.0 %while.16 = (s32[]{:T(128)}, f32[4,4,128]{2,1,0:T(4,128)S(1)}, f32[4,4,128]{2,1,0:T(4,128)S(1)}, f32[128,4,4,128]{3,0,2,1:T(8,128)S(1)}, s32[2,512]{1,0:T(2,128)...) while((s32[]{:T(128)}, f32[4,4,128]{2,1,0:T(4,128)S(1)}, ...), condition=%wide.region_8.9_spmd.clone, body=%wide.region_2.8_spmd.clone.sunk | while | flops 551100160 | bytes 20852624 | solution.py:61
  66.2 0.7 fusion.52
  68.2 5.0 %conditional.3 = ((f32[4,4,128]{2,1,0:T(4,128)S(1)}, f32[4,4,128]{2,1,0:T(4,128)S(1)}, f32[128,4,4,128]{3,0,2,1:T(8,128)S(1)})) conditional(s32[]{:T(128)} %convert_element_type.103, (s32[1,512]{1,0:T(1,128)S(1)}, s32[128]{0:T(128)S(1)}, bf16[2,512,4,128]{3,1,2,0:T(8,128)(2,1)S(1)}, s32[]{:T(128)}, bf16[128,4,4,128]{3,0,2,1:T(8,128)(2,1)S(1)}, ...), branch_computations={%region_4.6_spmd.clone, %region_7.7_spmd} | conditional | flops 551099520 | bytes 20846672 | solution.py:39
  68.2 1.3 %fusion.24 = s32[128]{0:T(128)S(1)} fusion(s32[128]{0:T(128)S(1)} %get-tuple-element.268, s32[128]{0:T(128)S(1)} %get-tuple-element.267, s32[128]{0:T(128)S(1)} %get-tuple-element.272, s32[128]{0:T(128)S(1)} %get-tuple-element.272, s32[128]{0:T(128)S(1)} %get-tuple-element.272, s32[128]{0:T(128)S(1)} %get-tuple-element.272, s32[]{:T(128)} %get-tuple-element.273, ...), kind=kLoop, calls=%fused_computation.25 | loop fusion | flops 1152 | bytes 3596 | tf_op jit(solution)/shard_map/add | solution.py:87
  69.7 0.8 fusion.2
  70.4 1.0 %fusion.4 = f32[4,4,128]{2,1,0:T(4,128)S(1)} fusion(f32[4,512,128,4]{2,1,3,0:T(8,128)S(1)} %get-tuple-element.320, f32[4,4,128]{2,1,0:T(4,128)S(1)} %get-tuple-element.400, pred[128,512]{0,1:T(8,128)(4,1)S(1)} %broadcast_compare_fusion), kind=kLoop, calls=%fused_computation.5 | loop fusion | flops 5240832 | bytes 4276224 | tf_op jit(solution)/shard_map/while/body/eval_jaxpr/cond/branch_0_fun/reduce_sum | solution.py:30
  71.5 1.7 %fusion.11 = f32[128,4,4,128]{3,0,2,1:T(8,128)S(1)} fusion(f32[4,512,128,4]{2,1,3,0:T(8,128)S(1)} %get-tuple-element.320, f32[4,4,128]{2,1,0:T(4,128)S(1)} %get-tuple-element.400, pred[128,512]{0,1:T(8,128)(4,1)S(1)} %broadcast_compare_fusion, f32[128,4,4,128]{3,0,2,1:T(8,128)S(1)} %get-tuple-element.261, bf16[2,512,4,128]{3,1,2,0:T(8,128)(2,1)S(1)} %copy-done.2, ...), kind=kOutput, calls=%fused_computation.9 | convolution fusion | flops 274202624 | bytes 6897668 | tf_op jit(solution)/shard_map/while/body/eval_jaxpr/cond/branch_0_fun/kgrs,skd->rkgd/dot_general | solution.py:32
  73.2 0.7 fusion.52
  75.2 5.0 %conditional.3 = ((f32[4,4,128]{2,1,0:T(4,128)S(1)}, f32[4,4,128]{2,1,0:T(4,128)S(1)}, f32[128,4,4,128]{3,0,2,1:T(8,128)S(1)})) conditional(s32[]{:T(128)} %convert_element_type.103, (s32[1,512]{1,0:T(1,128)S(1)}, s32[128]{0:T(128)S(1)}, bf16[2,512,4,128]{3,1,2,0:T(8,128)(2,1)S(1)}, s32[]{:T(128)}, bf16[128,4,4,128]{3,0,2,1:T(8,128)(2,1)S(1)}, ...), branch_computations={%region_4.6_spmd.clone, %region_7.7_spmd} | conditional | flops 551099520 | bytes 20846672 | solution.py:39
  75.3 1.3 %fusion.24 = s32[128]{0:T(128)S(1)} fusion(s32[128]{0:T(128)S(1)} %get-tuple-element.268, s32[128]{0:T(128)S(1)} %get-tuple-element.267, s32[128]{0:T(128)S(1)} %get-tuple-element.272, s32[128]{0:T(128)S(1)} %get-tuple-element.272, s32[128]{0:T(128)S(1)} %get-tuple-element.272, s32[128]{0:T(128)S(1)} %get-tuple-element.272, s32[]{:T(128)} %get-tuple-element.273, ...), kind=kLoop, calls=%fused_computation.25 | loop fusion | flops 1152 | bytes 3596 | tf_op jit(solution)/shard_map/add | solution.py:87
  76.7 0.8 fusion.2
  77.5 1.0 %fusion.4 = f32[4,4,128]{2,1,0:T(4,128)S(1)} fusion(f32[4,512,128,4]{2,1,3,0:T(8,128)S(1)} %get-tuple-element.320, f32[4,4,128]{2,1,0:T(4,128)S(1)} %get-tuple-element.400, pred[128,512]{0,1:T(8,128)(4,1)S(1)} %broadcast_compare_fusion), kind=kLoop, calls=%fused_computation.5 | loop fusion | flops 5240832 | bytes 4276224 | tf_op jit(solution)/shard_map/while/body/eval_jaxpr/cond/branch_0_fun/reduce_sum | solution.py:30
  78.5 1.7 %fusion.11 = f32[128,4,4,128]{3,0,2,1:T(8,128)S(1)} fusion(f32[4,512,128,4]{2,1,3,0:T(8,128)S(1)} %get-tuple-element.320, f32[4,4,128]{2,1,0:T(4,128)S(1)} %get-tuple-element.400, pred[128,512]{0,1:T(8,128)(4,1)S(1)} %broadcast_compare_fusion, f32[128,4,4,128]{3,0,2,1:T(8,128)S(1)} %get-tuple-element.261, bf16[2,512,4,128]{3,1,2,0:T(8,128)(2,1)S(1)} %copy-done.2, ...), kind=kOutput, calls=%fused_computation.9 | convolution fusion | flops 274202624 | bytes 6897668 | tf_op jit(solution)/shard_map/while/body/eval_jaxpr/cond/branch_0_fun/kgrs,skd->rkgd/dot_general | solution.py:32
  80.2 0.3 divide_convert_fusion
  80.6 0.4 copy.24
  81.0 1.2 %convert_element_type.46 = bf16[1,128,2048]{2,1,0:T(8,128)(2,1)} reshape(bf16[128,4,4,128]{3,2,1,0:T(4,128)(2,1)S(1)} %copy.24) | data formatting | bytes 1048576 | tf_op jit(solution)/shard_map/convert_element_type | solution.py:99
  82.2 0.6 log_add_fusion
  (38 shorter events, 0.7 us)
Async XLA Ops:
  7.2 53.3 %copy-start = (bf16[1,128,4096]{2,1,0:T(8,128)(2,1)S(1)}, bf16[1,128,4096]{2,1,0:T(8,128)(2,1)}, u32[]{:S(2)}) copy-start(bf16[1,128,4096]{2,1,0:T(8,128)(2,1)} %param.15) | copy-start | bytes 3145732
  7.2 53.3 %copy-start.1 = (bf16[1,128,4096]{2,1,0:T(8,128)(2,1)S(1)}, bf16[1,128,4096]{2,1,0:T(8,128)(2,1)}, u32[]{:S(2)}) copy-start(bf16[1,128,4096]{2,1,0:T(8,128)(2,1)} %param.16) | copy-start | bytes 3145732
  7.2 53.3 %copy-start.3 = (f32[4096]{0:T(1024)S(1)}, f32[4096]{0:T(1024)}, u32[]{:S(2)}) copy-start(f32[4096]{0:T(1024)} %param.17) | copy-start | bytes 49156
  7.2 54.9 %all-gather.3.cloned.1.call-start = ((), (), s32[]{:S(2)}) async-start(), calls=%async_computation | async-start | bytes 1179648 | tf_op jit(solution)/shard_map/all_gather | solution.py:93
  7.9 55.6 %all-gather.5.cloned.1.call-start = ((), (), s32[]{:S(2)}) async-start(), calls=%async_computation.1 | async-start | bytes 1179648 | tf_op jit(solution)/shard_map/all_gather | solution.py:94
  69.7 1.8 %copy-start.2 = (bf16[2,512,4,128]{3,1,2,0:T(8,128)(2,1)S(1)}, bf16[2,512,4,128]{3,1,2,0:T(8,128)(2,1)}, u32[]{:S(2)}) copy-start(bf16[2,512,4,128]{3,1,2,0:T(8,128)(2,1)} %get-tuple-element.262) | copy-start | bytes 3145732 | tf_op jit(solution)/shard_map/while/body/eval_jaxpr/cond
  76.7 1.8 %copy-start.2 = (bf16[2,512,4,128]{3,1,2,0:T(8,128)(2,1)S(1)}, bf16[2,512,4,128]{3,1,2,0:T(8,128)(2,1)}, u32[]{:S(2)}) copy-start(bf16[2,512,4,128]{3,1,2,0:T(8,128)(2,1)} %get-tuple-element.262) | copy-start | bytes 3145732 | tf_op jit(solution)/shard_map/while/body/eval_jaxpr/cond
Sparse Core Ops, SparseCore 0:
  9.9 25.9 all-gather.2
  37.7 23.9 all-gather.4
where the time goes:
time: 90.1 us; the launch traced here: 89.6 us
  blocking collectives  42.3 us (47%)
  other arithmetic  15.4 us (17%)
  between operations  14.2 us (16%)
  local copies, waits for them, and re-layouts  8.61 us (10%)
  matrix products  4.87 us (5%)
  loops' own time  2.82 us (3%)
  waiting for transfers between devices  1.4 us (2%)
    psum x1, blocking collectives, norm_backward(): gain_grad = lax.psum(partial_grad, ('ctx', 'dp'))  42.3 us
    dot_general x2, matrix products, dense_update(): jnp.einsum('kgrs,skd->rkgd', probs, value_rows, preferred_element_type=jn...  3.37 us
    unnamed x10, local copies, waits for them, and re-layouts  2.88 us
    another operation x1, loops' own time, fold_piece(): lax.scan(step_fn, carry, (key_rows.reshape(steps, block, heads, HEAD_WIDT...  2.66 us
    add x2, other arithmetic, attention(): jnp.where(local < half, mine[0], mine[1]) * half + local % half  2.54 us
    reduce_sum x1, other arithmetic, norm_backward(): partial_grad = jnp.sum(grad_f * normed, axis=0)  2.36 us
    reduce_sum x2, other arithmetic, dense_update(): total = total * factor + jnp.sum(weights, axis=-1)  2.02 us
    reduce_max x1, other arithmetic, update(): later = jnp.min(k_positions) > jnp.max(q_positions)  1.93 us
  transfers between devices with their start and end apart: 2, of which 0 were waited for; matrix products, arithmetic and copies ran while one was open for 14% of the time, Pallas kernels for 0%

commit v1 on v0

--- a/solution.py
+++ b/solution.py
@@ -107,7 +107,7 @@
     inv_rms = 1.0 / jnp.sqrt(jnp.mean(resid_f * resid_f, axis=-1, keepdims=True) + 1e-05)
     normed = resid_f * inv_rms
     partial_grad = jnp.sum(grad_f * normed, axis=0)
-    gain_grad = lax.psum(partial_grad, ("ctx", "dp"))
+    gain_grad = jnp.sum(lax.all_gather(partial_grad, ("ctx", "dp")), axis=0)
     scaled = gain[None, :] * grad_f
     resid_grad = (
         (scaled - normed * jnp.mean(scaled * normed, axis=-1, keepdims=True)) * inv_rms

time: 90.1 us -> 124 us (1.38)
  the two profiles are of different devices: /device:TPU:1 before, /device:TPU:0 now
where the time goes in v1:
time: 124 us
  blocking collectives  74.1 us (60%)
  other arithmetic  17.1 us (14%)
  between operations  14.2 us (11%)
  local copies, waits for them, and re-layouts  9.5 us (8%)
  matrix products  4.87 us (4%)
  loops' own time  2.82 us (2%)
  waiting for transfers between devices  1.4 us (1%)
    all_gather x1, blocking collectives, norm_backward(): gain_grad = jnp.sum(lax.all_gather(partial_grad, ('ctx', 'dp')), axis=0)  74.1 us
    dot_general x2, matrix products, dense_update(): jnp.einsum('kgrs,skd->rkgd', probs, value_rows, preferred_element_type=jn...  3.37 us
    unnamed x10, local copies, waits for them, and re-layouts  2.88 us
    another operation x1, loops' own time, fold_piece(): lax.scan(step_fn, carry, (key_rows.reshape(steps, block, heads, HEAD_WIDT...  2.66 us
    add x2, other arithmetic, attention(): jnp.where(local < half, mine[0], mine[1]) * half + local % half  2.54 us
  transfers between devices with their start and end apart: 2, of which 0 were waited for; matrix products, arithmetic and copies ran while one was open for 12% of the time, Pallas kernels for 0%

profile of v1, /device:TPU:0, one launch (start us, length us, event | category | flops | bytes accessed | tf_op | source)
XLA Modules:
  0.0 124.1 jit_solution(17511633943831182959)
XLA Ops:
  7.2 0.7 all-gather.4.cloned.1.call-update
  8.0 0.7 all-gather.6.cloned.1.call-update
  8.7 1.5 %fusion.38 = f32[128]{0:T(128)S(1)} fusion(bf16[1,128,4096]{2,1,0:T(8,128)(2,1)} %param.15), kind=kLoop, calls=%fused_computation.45 | loop fusion | flops 1572736 | bytes 1049088 | tf_op jit(solution)/shard_map/reduce_sum | solution.py:107
  10.2 0.7 select_reduce_fusion
  11.0 2.4 %fusion.34 = (f32[4096]{0:T(1024)S(1)}, f32[128]{0:T(128)S(1)}) fusion(bf16[1,128,4096]{2,1,0:T(8,128)(2,1)} %param.15, bf16[1,128,4096]{2,1,0:T(8,128)(2,1)} %param.16, f32[128]{0:T(128)S(1)} %add_rsqrt_fusion, f32[4096]{0:T(1024)} %param.17), kind=kLoop, calls=%fused_computation.41 | loop fusion | flops 4190080 | bytes 2130944 | tf_op jit(solution)/shard_map/reduce_sum | solution.py:109
  13.3 0.7 dynamic_slice.27
  14.1 1.3 %copy.26 = bf16[1,128,2048]{1,2,0:T(8,128)(2,1)S(1)} copy(bf16[1,128,2048]{2,1,0:T(8,128)(2,1)} %param.11) | data formatting | bytes 1048576 | tf_op args[0]
  15.7 74.1 %all-gather = f32[131072]{0:T(1024)S(1)} all-gather(f32[4096]{0:T(1024)S(1)} %get-tuple-element.302), channel_id=2, replica_groups=mesh['ctx'=8,'dp'=4] {'ctx','dp'}, dimensions={0}, use_global_device_ids=true | all-gather | bytes 540672 | tf_op jit(solution)/shard_map/all_gather | solution.py:110
  89.8 0.9 reshape.127
  90.7 1.7 %reduce_sum.60 = f32[4096]{0:T(1024)} reduce(f32[32,4096]{1,0:T(8,128)} %reshape.127, f32[]{:T(128)} %constant.97.clone.1), dimensions={0}, to_apply=%region_12.13 | reduce | flops 126976 | bytes 540676 | tf_op jit(solution)/shard_map/reduce_sum | solution.py:110
  92.4 0.6 fusion.49
  93.0 1.9 %fusion.47 = s32[]{:T(128)} fusion(s32[]{:T(128)} %bitcast.11, s32[]{:T(128)} %bitcast.10), kind=kLoop, calls=%fused_computation.69 | loop fusion | flops 1407 | bytes 12 | tf_op jit(solution)/shard_map/while/body/eval_jaxpr/reduce_max | solution.py:38
  95.0 1.5 %fusion.37 = bf16[1,128,4096]{2,1,0:T(8,128)(2,1)} fusion(bf16[1,128,4096]{2,1,0:T(8,128)(2,1)S(1)} %copy-done.1, bf16[1,128,4096]{2,1,0:T(8,128)(2,1)S(1)} %copy-done, f32[128]{0:T(128)S(1)} %broadcast_multiply_fusion.1, f32[128]{0:T(128)S(1)} %add_rsqrt_fusion, f32[4096]{0:T(1024)S(1)} %copy-done.3), kind=kLoop, calls=%fused_computation.44 | loop fusion | flops 4194304 | bytes 3163136 | tf_op jit(solution)/shard_map/convert_element_type | solution.py:114
  96.5 1.3 %reshape_reshape_squeeze.6 = bf16[2,512,4,128]{3,2,1,0:T(4,128)(2,1)S(1)} reshape(bf16[1,1024,512]{2,1,0:T(8,128)(2,1)} %all-gather.4.cloned.1.call-done) | data formatting | bytes 2097152 | tf_op jit(solution)/shard_map/reshape;reshape;squeeze | solution.py:65
  98.0 1.3 %reshape_reshape_squeeze.7 = bf16[2,512,4,128]{3,2,1,0:T(4,128)(2,1)S(1)} reshape(bf16[1,1024,512]{2,1,0:T(8,128)(2,1)} %all-gather.6.cloned.1.call-done) | data formatting | bytes 2097152 | tf_op jit(solution)/shard_map/reshape;reshape;squeeze | solution.py:66
  99.4 1.1 copy.29
  100.6 14.0 %while.16 = (s32[]{:T(128)}, f32[4,4,128]{2,1,0:T(4,128)S(1)}, f32[4,4,128]{2,1,0:T(4,128)S(1)}, f32[128,4,4,128]{3,0,2,1:T(8,128)S(1)}, s32[2,512]{1,0:T(2,128)...) while((s32[]{:T(128)}, f32[4,4,128]{2,1,0:T(4,128)S(1)}, ...), condition=%wide.region_8.9_spmd.clone, body=%wide.region_2.8_spmd.clone.sunk | while | flops 551100160 | bytes 20852624 | solution.py:61
  100.7 0.7 fusion.52
  102.7 5.0 %conditional.3 = ((f32[4,4,128]{2,1,0:T(4,128)S(1)}, f32[4,4,128]{2,1,0:T(4,128)S(1)}, f32[128,4,4,128]{3,0,2,1:T(8,128)S(1)})) conditional(s32[]{:T(128)} %convert_element_type.103, (s32[1,512]{1,0:T(1,128)S(1)}, s32[128]{0:T(128)S(1)}, bf16[2,512,4,128]{3,1,2,0:T(8,128)(2,1)S(1)}, s32[]{:T(128)}, bf16[128,4,4,128]{3,0,2,1:T(8,128)(2,1)S(1)}, ...), branch_computations={%region_4.6_spmd.clone, %region_7.7_spmd} | conditional | flops 551099520 | bytes 20846672 | solution.py:39
  102.7 1.3 %fusion.24 = s32[128]{0:T(128)S(1)} fusion(s32[128]{0:T(128)S(1)} %get-tuple-element.279, s32[128]{0:T(128)S(1)} %get-tuple-element.278, s32[128]{0:T(128)S(1)} %get-tuple-element.283, s32[128]{0:T(128)S(1)} %get-tuple-element.283, s32[128]{0:T(128)S(1)} %get-tuple-element.283, s32[128]{0:T(128)S(1)} %get-tuple-element.283, s32[]{:T(128)} %get-tuple-element.284, ...), kind=kLoop, calls=%fused_computation.25 | loop fusion | flops 1152 | bytes 3596 | tf_op jit(solution)/shard_map/add | solution.py:87
  104.1 0.8 fusion.2
  104.9 1.0 fusion.4
  105.9 1.7 %fusion.11 = f32[128,4,4,128]{3,0,2,1:T(8,128)S(1)} fusion(f32[4,512,128,4]{2,1,3,0:T(8,128)S(1)} %get-tuple-element.331, f32[4,4,128]{2,1,0:T(4,128)S(1)} %get-tuple-element.411, pred[128,512]{0,1:T(8,128)(4,1)S(1)} %broadcast_compare_fusion, f32[128,4,4,128]{3,0,2,1:T(8,128)S(1)} %get-tuple-element.272, bf16[2,512,4,128]{3,1,2,0:T(8,128)(2,1)S(1)} %copy-done.2, ...), kind=kOutput, calls=%fused_computation.9 | convolution fusion | flops 274202624 | bytes 6897668 | tf_op jit(solution)/shard_map/while/body/eval_jaxpr/cond/branch_0_fun/kgrs,skd->rkgd/dot_general | solution.py:32
  107.7 0.7 fusion.52
  109.7 5.0 %conditional.3 = ((f32[4,4,128]{2,1,0:T(4,128)S(1)}, f32[4,4,128]{2,1,0:T(4,128)S(1)}, f32[128,4,4,128]{3,0,2,1:T(8,128)S(1)})) conditional(s32[]{:T(128)} %convert_element_type.103, (s32[1,512]{1,0:T(1,128)S(1)}, s32[128]{0:T(128)S(1)}, bf16[2,512,4,128]{3,1,2,0:T(8,128)(2,1)S(1)}, s32[]{:T(128)}, bf16[128,4,4,128]{3,0,2,1:T(8,128)(2,1)S(1)}, ...), branch_computations={%region_4.6_spmd.clone, %region_7.7_spmd} | conditional | flops 551099520 | bytes 20846672 | solution.py:39
  109.7 1.3 %fusion.24 = s32[128]{0:T(128)S(1)} fusion(s32[128]{0:T(128)S(1)} %get-tuple-element.279, s32[128]{0:T(128)S(1)} %get-tuple-element.278, s32[128]{0:T(128)S(1)} %get-tuple-element.283, s32[128]{0:T(128)S(1)} %get-tuple-element.283, s32[128]{0:T(128)S(1)} %get-tuple-element.283, s32[128]{0:T(128)S(1)} %get-tuple-element.283, s32[]{:T(128)} %get-tuple-element.284, ...), kind=kLoop, calls=%fused_computation.25 | loop fusion | flops 1152 | bytes 3596 | tf_op jit(solution)/shard_map/add | solution.py:87
  111.1 0.8 fusion.2
  111.9 1.0 fusion.4
  112.9 1.7 %fusion.11 = f32[128,4,4,128]{3,0,2,1:T(8,128)S(1)} fusion(f32[4,512,128,4]{2,1,3,0:T(8,128)S(1)} %get-tuple-element.331, f32[4,4,128]{2,1,0:T(4,128)S(1)} %get-tuple-element.411, pred[128,512]{0,1:T(8,128)(4,1)S(1)} %broadcast_compare_fusion, f32[128,4,4,128]{3,0,2,1:T(8,128)S(1)} %get-tuple-element.272, bf16[2,512,4,128]{3,1,2,0:T(8,128)(2,1)S(1)} %copy-done.2, ...), kind=kOutput, calls=%fused_computation.9 | convolution fusion | flops 274202624 | bytes 6897668 | tf_op jit(solution)/shard_map/while/body/eval_jaxpr/cond/branch_0_fun/kgrs,skd->rkgd/dot_general | solution.py:32
  115.0 0.4 copy.30
  115.4 1.2 convert_element_type.46
  116.6 0.6 log_add_fusion
  (40 shorter events, 1.4 us)
Async XLA Ops:
  7.2 87.8 %copy-start = (bf16[1,128,4096]{2,1,0:T(8,128)(2,1)S(1)}, bf16[1,128,4096]{2,1,0:T(8,128)(2,1)}, u32[]{:S(2)}) copy-start(bf16[1,128,4096]{2,1,0:T(8,128)(2,1)} %param.15) | copy-start | bytes 3145732
  7.2 87.8 %copy-start.1 = (bf16[1,128,4096]{2,1,0:T(8,128)(2,1)S(1)}, bf16[1,128,4096]{2,1,0:T(8,128)(2,1)}, u32[]{:S(2)}) copy-start(bf16[1,128,4096]{2,1,0:T(8,128)(2,1)} %param.16) | copy-start | bytes 3145732
  7.2 87.8 %copy-start.3 = (f32[4096]{0:T(1024)S(1)}, f32[4096]{0:T(1024)}, u32[]{:S(2)}) copy-start(f32[4096]{0:T(1024)} %param.17) | copy-start | bytes 49156
  7.2 89.3 %all-gather.4.cloned.1.call-start = ((), (), s32[]{:S(2)}) async-start(), calls=%async_computation | async-start | bytes 1179648 | tf_op jit(solution)/shard_map/all_gather | solution.py:93
  7.9 90.1 %all-gather.6.cloned.1.call-start = ((), (), s32[]{:S(2)}) async-start(), calls=%async_computation.1 | async-start | bytes 1179648 | tf_op jit(solution)/shard_map/all_gather | solution.py:94
  104.1 1.8 %copy-start.2 = (bf16[2,512,4,128]{3,1,2,0:T(8,128)(2,1)S(1)}, bf16[2,512,4,128]{3,1,2,0:T(8,128)(2,1)}, u32[]{:S(2)}) copy-start(bf16[2,512,4,128]{3,1,2,0:T(8,128)(2,1)} %get-tuple-element.273) | copy-start | bytes 3145732 | tf_op jit(solution)/shard_map/while/body/eval_jaxpr/cond
  111.1 1.8 %copy-start.2 = (bf16[2,512,4,128]{3,1,2,0:T(8,128)(2,1)S(1)}, bf16[2,512,4,128]{3,1,2,0:T(8,128)(2,1)}, u32[]{:S(2)}) copy-start(bf16[2,512,4,128]{3,1,2,0:T(8,128)(2,1)} %get-tuple-element.273) | copy-start | bytes 3145732 | tf_op jit(solution)/shard_map/while/body/eval_jaxpr/cond
Sparse Core Ops, SparseCore 0:
  9.9 26.2 all-gather.3
  38.1 23.6 all-gather.5
